TPU v7x, 32 devices: a whole 2x2x4 slice. The times are simulated.
32 devices in a mesh: dp: 8 (over y, x, core), tensor: 4 (over z).
Axes of the slice: x: 2, y: 2, z: 4, core: 2. Of those that a mesh axis runs over, the one named last changes fastest.
Arguments:
- tokens: bfloat16 [8192, 1280], P(('dp', 'tensor')), may hold values from -6 to 6
- w_query: bfloat16 [1280, 1280], P('dp', 'tensor'), may hold values from -0.15625 to 0.15625
- w_key: bfloat16 [1280, 1280], P('dp', 'tensor'), may hold values from -0.15625 to 0.15625
- w_value: bfloat16 [1280, 1280], P('dp', 'tensor'), may hold values from -0.15625 to 0.15625
- w_out: bfloat16 [1280, 1280], P('dp', 'tensor'), may hold values from -0.15625 to 0.15625
- w_up: bfloat16 [1280, 5120], P('dp', 'tensor'), may hold values from -0.15625 to 0.15625
- w_gate: bfloat16 [1280, 5120], P('dp', 'tensor'), may hold values from -0.15625 to 0.15625
- w_down: bfloat16 [1280, 5120], P('dp', 'tensor'), may hold values from -0.078125 to 0.078125
- qk_scale: float32 [1280], P('tensor'), may hold values from 0.8 to 1.8
- up_scale: float32 [5120], P('tensor'), may hold values from 0.5 to 2
- gate_scale: float32 [5120], P('tensor'), may hold values from 0.5 to 2
- alpha_attn: float32 [1280], replicated, may hold values from 0.2 to 0.6
- alpha_mlp: float32 [1280], replicated, may hold values from 0.2 to 0.6
- cotangent: bfloat16 [8192, 1280], P(('dp', 'tensor')), may hold values from -6 to 6
Outputs:
- output: bfloat16 [8192, 1280], P(('dp', 'tensor'))
- tokens_gradient: float32 [8192, 1280], P(('dp', 'tensor'))
- w_query_gradient: float32 [1280, 1280], P('dp', 'tensor')
- w_key_gradient: float32 [1280, 1280], P('dp', 'tensor')
- w_value_gradient: float32 [1280, 1280], P('dp', 'tensor')
- w_out_gradient: float32 [1280, 1280], P('dp', 'tensor')
- w_up_gradient: float32 [1280, 5120], P('dp', 'tensor')
- w_gate_gradient: float32 [1280, 5120], P('dp', 'tensor')
- w_down_gradient: float32 [1280, 5120], P('dp', 'tensor')
- qk_scale_gradient: float32 [1280], P('tensor')
- up_scale_gradient: float32 [5120], P('tensor')
- gate_scale_gradient: float32 [5120], P('tensor')
- alpha_attn_gradient: float32 [1280], replicated
- alpha_mlp_gradient: float32 [1280], replicated
All inputs are finite; a program needn't handle non-finite values.
Results may differ from a plain program's by a relative error of at most 0.017.
Values may be sent and summed in bfloat16 or wider, within the bound.
A program may use at most 192 MiB of HBM per device.

v0:
```python
import jax
import jax.numpy as jnp
from jax import lax
from jax.sharding import PartitionSpec as P

HEAD_DIM = 64
HIGH = lax.Precision.HIGHEST
EPS = 1e-06


def unit_rows(value):
    scale = lax.rsqrt(jnp.mean(value * value, axis=-1, keepdims=True) + EPS)
    return (value * scale, scale)


def unit_back(grad, unit, scale):
    return scale * (grad - unit * jnp.mean(grad * unit, axis=-1, keepdims=True))


def contract_rows(left, right):
    return lax.dot_general(
        left, right, (((0,), (0,)), ((), ())), preferred_element_type=jnp.float32
    )


def contract_cols(left, right):
    return lax.dot_general(
        left, right, (((1,), (1,)), ((), ())), preferred_element_type=jnp.float32
    )


def tables(width, length):
    half_dim = HEAD_DIM // 2
    column = lax.iota(jnp.int32, width)
    within = column % HEAD_DIM
    freq_index = (within % half_dim).astype(jnp.float32)
    frequency = 10000.0 ** (-freq_index / half_dim)
    position = lax.iota(jnp.float32, length)
    angle = position[:, None] * frequency[None, :]
    first_half = (within < half_dim)[None, :]
    heads = width // HEAD_DIM
    member = (
        lax.broadcasted_iota(jnp.int32, (width, heads), 0) // HEAD_DIM
        == lax.broadcasted_iota(jnp.int32, (width, heads), 1)
    ).astype(jnp.float32)
    return (jnp.cos(angle), jnp.sin(angle), first_half, member)


def rope_apply(value, cosine, sine, first_half):
    half_dim = HEAD_DIM // 2
    turned = jnp.where(
        first_half, -jnp.roll(value, -half_dim, axis=1), jnp.roll(value, half_dim, axis=1)
    )
    return value * cosine + turned * sine


def rope_back(grad, cosine, sine, first_half):
    half_dim = HEAD_DIM // 2
    weighted = grad * sine
    turned = jnp.where(
        first_half, jnp.roll(weighted, -half_dim, axis=1), -jnp.roll(weighted, half_dim, axis=1)
    )
    return grad * cosine + turned


def head_unit(value, member):
    mean_sq = (
        jnp.dot(value * value, member, precision=HIGH, preferred_element_type=jnp.float32)
        / HEAD_DIM
    )
    scale = jnp.dot(
        lax.rsqrt(mean_sq + EPS), member.T, precision=HIGH, preferred_element_type=jnp.float32
    )
    return (value * scale, scale)


def head_back(grad, unit, scale, member):
    inner = (
        jnp.dot(grad * unit, member, precision=HIGH, preferred_element_type=jnp.float32) / HEAD_DIM
    )
    spread = jnp.dot(inner, member.T, precision=HIGH, preferred_element_type=jnp.float32)
    return scale * (grad - unit * spread)


def block_scores(query3, key3, start, stop, block):
    scale = HEAD_DIM ** (-0.5)
    scores = (
        jnp.einsum(
            "qhd,khd->hqk", query3[start:stop], key3[:stop], preferred_element_type=jnp.float32
        )
        * scale
    )
    allowed = start + lax.broadcasted_iota(jnp.int32, (block, stop), 0) >= lax.broadcasted_iota(
        jnp.int32, (block, stop), 1
    )
    return jnp.where(allowed[None], scores, -jnp.inf)


def attend(query3, key3, value3, block):
    length = query3.shape[0]
    outputs = []
    totals = []
    for block_id in range(length // block):
        start = block_id * block
        stop = start + block
        scores = block_scores(query3, key3, start, stop, block)
        row_max = jnp.max(scores, axis=-1, keepdims=True)
        log_total = jnp.log(jnp.sum(jnp.exp(scores - row_max), axis=-1, keepdims=True)) + row_max
        weights = jnp.exp(scores - log_total).astype(jnp.bfloat16)
        outputs.append(
            jnp.einsum("hqk,khd->qhd", weights, value3[:stop], preferred_element_type=jnp.float32)
        )
        totals.append(log_total)
    return (jnp.concatenate(outputs, axis=0), totals)


def attend_back(query3, key3, value3, grad3, totals, block):
    length = query3.shape[0]
    scale = HEAD_DIM ** (-0.5)
    query_parts = []
    key_grad = jnp.zeros(key3.shape, jnp.float32)
    value_grad = jnp.zeros(value3.shape, jnp.float32)
    for block_id in range(length // block):
        start = block_id * block
        stop = start + block
        scores = block_scores(query3, key3, start, stop, block)
        probs = jnp.exp(scores - totals[block_id])
        g_probs = jnp.einsum(
            "qhd,khd->hqk", grad3[start:stop], value3[:stop], preferred_element_type=jnp.float32
        )
        inner = jnp.sum(probs * g_probs, axis=-1, keepdims=True)
        g_scores = (probs * (g_probs - inner)).astype(jnp.bfloat16)
        query_parts.append(
            jnp.einsum("hqk,khd->qhd", g_scores, key3[:stop], preferred_element_type=jnp.float32)
            * scale
        )
        key_grad = key_grad.at[:stop].add(
            jnp.einsum(
                "hqk,qhd->khd", g_scores, query3[start:stop], preferred_element_type=jnp.float32
            )
            * scale
        )
        value_grad = value_grad.at[:stop].add(
            jnp.einsum(
                "hqk,qhd->khd",
                probs.astype(jnp.bfloat16),
                grad3[start:stop],
                preferred_element_type=jnp.float32,
            )
        )
    return (jnp.concatenate(query_parts, axis=0), key_grad, value_grad)


def gather_attention(w_query, w_key, w_value, w_out):
    return (
        lax.all_gather(w_query, "dp", axis=0, tiled=True),
        lax.all_gather(w_key, "dp", axis=0, tiled=True),
        lax.all_gather(w_value, "dp", axis=0, tiled=True),
        lax.all_gather(w_out, "dp", axis=0, tiled=True),
    )


def gather_feedforward(w_up, w_gate, w_down):
    return (
        lax.all_gather(w_up, "dp", axis=0, tiled=True),
        lax.all_gather(w_gate, "dp", axis=0, tiled=True),
        lax.all_gather(w_down, "dp", axis=0, tiled=True),
    )


def on_device(
    tokens,
    w_query,
    w_key,
    w_value,
    w_out,
    w_up,
    w_gate,
    w_down,
    qk_scale,
    up_scale,
    gate_scale,
    alpha_attn,
    alpha_mlp,
    cotangent,
):
    query_w, key_w, value_w, out_w = gather_attention(w_query, w_key, w_value, w_out)
    whole = lax.all_gather(tokens, "tensor", axis=0, tiled=True)
    length = whole.shape[0]
    width = query_w.shape[1]
    block = min(512, length)
    cosine, sine, first_half, member = tables(width, length)
    shape3 = (length, width // HEAD_DIM, HEAD_DIM)
    q_raw = jnp.dot(whole, query_w, preferred_element_type=jnp.float32)
    k_raw = jnp.dot(whole, key_w, preferred_element_type=jnp.float32)
    value_low = jnp.dot(whole, value_w, preferred_element_type=jnp.float32).astype(jnp.bfloat16)
    q_unit, q_norm = head_unit(rope_apply(q_raw, cosine, sine, first_half), member)
    k_unit, k_norm = head_unit(rope_apply(k_raw, cosine, sine, first_half), member)
    query_low = (q_unit * qk_scale).astype(jnp.bfloat16)
    key_low = (k_unit * qk_scale).astype(jnp.bfloat16)
    query3 = query_low.reshape(shape3)
    key3 = key_low.reshape(shape3)
    value3 = value_low.reshape(shape3)
    attended, totals = attend(query3, key3, value3, block)
    attended_low = attended.reshape(length, width).astype(jnp.bfloat16)
    attn_sum = lax.psum_scatter(
        contract_cols(attended_low, out_w), "tensor", scatter_dimension=0, tiled=True
    )
    attn_unit, attn_norm = unit_rows(attn_sum)
    residual = tokens.astype(jnp.float32)
    mid, mid_norm = unit_rows(residual + alpha_attn * (attn_unit - residual))
    mid_low = mid.astype(jnp.bfloat16)
    up_w, gate_w, down_w = gather_feedforward(w_up, w_gate, w_down)
    mid_whole = lax.all_gather(mid_low, "tensor", axis=0, tiled=True)
    up_sum = jnp.dot(mid_whole, up_w, preferred_element_type=jnp.float32)
    gate_sum = jnp.dot(mid_whole, gate_w, preferred_element_type=jnp.float32)
    up_val = up_sum * up_scale
    gate_val = gate_sum * gate_scale
    sigma = jax.nn.sigmoid(gate_val)
    hidden_low = (up_val * (gate_val * sigma)).astype(jnp.bfloat16)
    mlp_sum = lax.psum_scatter(
        contract_cols(hidden_low, down_w), "tensor", scatter_dimension=0, tiled=True
    )
    mlp_unit, mlp_norm = unit_rows(mlp_sum)
    final, final_norm = unit_rows(mid + alpha_mlp * (mlp_unit - mid))
    output = final.astype(jnp.bfloat16)
    g_second = unit_back(cotangent.astype(jnp.float32), final, final_norm)
    g_alpha_mlp = jnp.sum((mlp_unit - mid) * g_second, axis=0)
    g_mlp_low = unit_back(alpha_mlp * g_second, mlp_unit, mlp_norm).astype(jnp.bfloat16)
    up_w, gate_w, down_w = gather_feedforward(w_up, w_gate, w_down)
    g_mlp_whole = lax.all_gather(g_mlp_low, "tensor", axis=0, tiled=True)
    down_grad = contract_rows(g_mlp_whole, hidden_low)
    g_hidden = jnp.dot(g_mlp_whole, down_w, preferred_element_type=jnp.float32)
    g_up = g_hidden * (gate_val * sigma)
    g_gate = g_hidden * up_val * (sigma * (1.0 + gate_val * (1.0 - sigma)))
    up_scale_grad = jnp.sum(g_up * up_sum, axis=0)
    gate_scale_grad = jnp.sum(g_gate * gate_sum, axis=0)
    g_up_low = (g_up * up_scale).astype(jnp.bfloat16)
    g_gate_low = (g_gate * gate_scale).astype(jnp.bfloat16)
    up_grad = contract_rows(mid_whole, g_up_low)
    gate_grad = contract_rows(mid_whole, g_gate_low)
    g_mid_part = contract_cols(g_up_low, up_w) + contract_cols(g_gate_low, gate_w)
    g_mid = (1.0 - alpha_mlp) * g_second + lax.psum_scatter(
        g_mid_part, "tensor", scatter_dimension=0, tiled=True
    )
    up_grad, gate_grad, down_grad = (
        lax.psum_scatter(up_grad, "dp", scatter_dimension=0, tiled=True),
        lax.psum_scatter(gate_grad, "dp", scatter_dimension=0, tiled=True),
        lax.psum_scatter(down_grad, "dp", scatter_dimension=0, tiled=True),
    )
    g_first = unit_back(g_mid, mid, mid_norm)
    g_alpha_attn = jnp.sum((attn_unit - residual) * g_first, axis=0)
    g_attn_low = unit_back(alpha_attn * g_first, attn_unit, attn_norm).astype(jnp.bfloat16)
    query_w, key_w, value_w, out_w = gather_attention(w_query, w_key, w_value, w_out)
    g_attn_whole = lax.all_gather(g_attn_low, "tensor", axis=0, tiled=True)
    out_grad = contract_rows(g_attn_whole, attended_low)
    g_attended_low = jnp.dot(g_attn_whole, out_w, preferred_element_type=jnp.float32).astype(
        jnp.bfloat16
    )
    g_query3, g_key3, g_value3 = attend_back(
        query3, key3, value3, g_attended_low.reshape(shape3), totals, block
    )
    g_query = g_query3.reshape(length, width)
    g_key = g_key3.reshape(length, width)
    qk_grad = jnp.sum(g_query * q_unit, axis=0) + jnp.sum(g_key * k_unit, axis=0)
    g_q_raw_low = rope_back(
        head_back(g_query * qk_scale, q_unit, q_norm, member), cosine, sine, first_half
    ).astype(jnp.bfloat16)
    g_k_raw_low = rope_back(
        head_back(g_key * qk_scale, k_unit, k_norm, member), cosine, sine, first_half
    ).astype(jnp.bfloat16)
    g_value_low = g_value3.reshape(length, width).astype(jnp.bfloat16)
    query_grad = contract_rows(whole, g_q_raw_low)
    key_grad = contract_rows(whole, g_k_raw_low)
    value_grad = contract_rows(whole, g_value_low)
    g_tok_part = (
        contract_cols(g_q_raw_low, query_w)
        + contract_cols(g_k_raw_low, key_w)
        + contract_cols(g_value_low, value_w)
    )
    tokens_grad = (1.0 - alpha_attn) * g_first + lax.psum_scatter(
        g_tok_part.astype(jnp.bfloat16), "tensor", scatter_dimension=0, tiled=True
    ).astype(jnp.float32)
    query_grad, key_grad, value_grad, out_grad = (
        lax.psum_scatter(query_grad, "dp", scatter_dimension=0, tiled=True),
        lax.psum_scatter(key_grad, "dp", scatter_dimension=0, tiled=True),
        lax.psum_scatter(value_grad, "dp", scatter_dimension=0, tiled=True),
        lax.psum_scatter(out_grad, "dp", scatter_dimension=0, tiled=True),
    )
    qk_grad, up_scale_grad, gate_scale_grad = lax.psum(
        (qk_grad, up_scale_grad, gate_scale_grad), "dp"
    )
    g_alpha_attn, g_alpha_mlp = lax.psum((g_alpha_attn, g_alpha_mlp), ("dp", "tensor"))
    return (
        output,
        tokens_grad,
        query_grad,
        key_grad,
        value_grad,
        out_grad,
        up_grad,
        gate_grad,
        down_grad,
        qk_grad,
        up_scale_grad,
        gate_scale_grad,
        g_alpha_attn,
        g_alpha_mlp,
    )


def solution(mesh):
    in_specs = (
        P(("dp", "tensor"), None),
        P("dp", "tensor"),
        P("dp", "tensor"),
        P("dp", "tensor"),
        P("dp", "tensor"),
        P("dp", "tensor"),
        P("dp", "tensor"),
        P("dp", "tensor"),
        P("tensor"),
        P("tensor"),
        P("tensor"),
        P(),
        P(),
        P(("dp", "tensor"), None),
    )
    out_specs = (
        P(("dp", "tensor"), None),
        P(("dp", "tensor"), None),
        P("dp", "tensor"),
        P("dp", "tensor"),
        P("dp", "tensor"),
        P("dp", "tensor"),
        P("dp", "tensor"),
        P("dp", "tensor"),
        P("dp", "tensor"),
        P("tensor"),
        P("tensor"),
        P("tensor"),
        P(),
        P(),
    )
    return jax.shard_map(
        on_device, mesh=mesh, in_specs=in_specs, out_specs=out_specs, check_vma=False
    )
```

profile of v0, /device:TPU:0, one launch (start us, length us, event | category | flops | bytes accessed | tf_op | source)
XLA Modules:
  0.0 1157.3 jit_solution(15452497443347139287)
XLA Ops:
  9.0 12.8 %all_gather.41 = bf16[1280,320]{1,0:T(8,128)(2,1)S(1)} all-gather(bf16[160,320]{1,0:T(8,128)(2,1)} %param.29), channel_id=1, replica_groups=mesh['dp'=8,'tensor'=4] {'dp'}, dimensions={0}, use_global_device_ids=true | all-gather | bytes 921600 | tf_op jit(solution)/shard_map/all_gather | solution.py:158
  21.8 11.6 %all_gather.43 = bf16[1280,320]{1,0:T(8,128)(2,1)} all-gather(bf16[160,320]{1,0:T(8,128)(2,1)S(1)} %copy-done.50), channel_id=1, replica_groups=mesh['dp'=8,'tensor'=4] {'dp'}, dimensions={0}, use_global_device_ids=true | all-gather | bytes 921600 | tf_op jit(solution)/shard_map/all_gather | solution.py:157
  33.3 11.4 all_gather.42
  44.7 11.5 all_gather.44
  56.6 11.3 all-gather.8.cloned.1.call-done
  67.9 3.0 fusion.124
  74.3 6.5 fusion.20
  89.5 3.1 exponential_reduce_fusion
  96.0 2.9 fusion.67
  101.9 3.9 fusion.125
  106.4 92.1 %reduce-scatter.18.cloned.1.call-done = f32[256,1280]{1,0:T(8,128)} async-done(((f32[1024,1280]{1,0:T(8,128)}), f32[256,1280]{1,0:T(8,128)}) %reduce-scatter.18.cloned.1.call-update) | async-done | bytes 1310736 | tf_op jit(solution)/shard_map/reduce_scatter | solution.py:206
  204.5 53.4 %all-gather.10.cloned.1.call-done = bf16[1024,1280]{1,0:T(8,128)(2,1)} async-done(((bf16[256,1280]{1,0:T(8,128)(2,1)}), bf16[1024,1280]{1,0:T(8,128)(2,1)}) %all-gather.10.cloned.1.call-update) | async-done | bytes 2621456 | tf_op jit(solution)/shard_map/all_gather | solution.py:214
  257.8 8.6 fusion.126
  266.4 24.5 %all-gather.12.cloned.1.call-done = bf16[1280,1280]{1,0:T(8,128)(2,1)} async-done(((bf16[160,1280]{1,0:T(8,128)(2,1)}), bf16[1280,1280]{1,0:T(8,128)(2,1)}) %all-gather.12.cloned.1.call-update) | async-done | bytes 3276816 | tf_op jit(solution)/shard_map/all_gather | solution.py:165
  290.8 11.3 multiply_convert_fusion.4
  302.1 23.2 %all-gather.16.cloned.1.call-done = bf16[1280,1280]{1,0:T(8,128)(2,1)} async-done(((bf16[160,1280]{1,0:T(8,128)(2,1)}), bf16[1280,1280]{1,0:T(8,128)(2,1)}) %all-gather.16.cloned.1.call-update) | async-done | bytes 3276816 | tf_op jit(solution)/shard_map/all_gather | solution.py:167
  325.4 8.7 fusion.127
  334.1 93.9 %reduce-scatter.20.cloned.1.call-done = f32[256,1280]{1,0:T(8,128)} async-done(((f32[1024,1280]{1,0:T(8,128)}), f32[256,1280]{1,0:T(8,128)}) %reduce-scatter.20.cloned.1.call-update) | async-done | bytes 1310736 | tf_op jit(solution)/shard_map/reduce_scatter | solution.py:221
  435.4 54.5 %all-gather.18.cloned.1.call-done = bf16[1024,1280]{1,0:T(8,128)(2,1)} async-done(((bf16[256,1280]{1,0:T(8,128)(2,1)}), bf16[1024,1280]{1,0:T(8,128)(2,1)}) %all-gather.18.cloned.1.call-update) | async-done | bytes 2621456 | tf_op jit(solution)/shard_map/all_gather | solution.py:231
  490.0 11.1 multiply_reduce_fusion.1
  501.1 3.6 fusion.128
  505.5 5.4 convolution_add_fusion
  511.0 92.5 %reduce-scatter.22.cloned.1.call-done = f32[256,1280]{1,0:T(8,128)} async-done(((f32[1024,1280]{1,0:T(8,128)}), f32[256,1280]{1,0:T(8,128)}) %reduce-scatter.22.cloned.1.call-update) | async-done | bytes 1310736 | tf_op jit(solution)/shard_map/reduce_scatter | solution.py:243
  610.8 54.8 %all-gather.20.cloned.1.call-done = bf16[1024,1280]{1,0:T(8,128)(2,1)} async-done(((bf16[256,1280]{1,0:T(8,128)(2,1)}), bf16[1024,1280]{1,0:T(8,128)(2,1)}) %all-gather.20.cloned.1.call-update) | async-done | bytes 2621456 | tf_op jit(solution)/shard_map/all_gather | solution.py:255
  669.1 4.5 multiply_reduce_fusion.3
  673.7 4.2 multiply_convert_fusion.1
  680.1 3.9 multiply_reduce_fusion
  683.9 3.3 multiply_convert_fusion
  695.2 7.2 fusion.35
  705.3 6.0 fusion.24
  714.6 3.0 fusion.12
  718.4 3.3 add_convert_fusion
  721.9 8.9 fusion.132
  731.0 9.7 fusion.68
  740.8 8.8 fusion.133
  750.7 4.0 convolution_bitcast_fusion.2
  758.6 3.9 convolution_bitcast_fusion.1
  762.5 2.8 copy.48
  766.4 3.9 convolution_bitcast_fusion
  774.2 4.6 fusion.131
  778.8 39.5 %all-reduce.2 = (f32[1280]{0:T(1024)}, f32[1280]{0:T(1024)}) all-reduce(f32[1280]{0:T(1024)S(1)} %get-tuple-element.110, f32[1280]{0:T(1024)S(1)} %get-tuple-element.108), channel_id=1, replica_groups=mesh['dp'=8,'tensor'=4] {'dp','tensor'}, use_global_device_ids=true, to_apply=%region_33.34 | all-reduce | flops 2560 | bytes 20480 | tf_op jit(solution)/shard_map/psum | solution.py:293
  820.3 25.1 %all-reduce.3 = (f32[320]{0:T(512)}, f32[1280]{0:T(1024)}, f32[1280]{0:T(1024)}) all-reduce(f32[320]{0:T(512)S(1)} %add.253, f32[1280]{0:T(1024)S(1)} %get-tuple-element.107, f32[1280]{0:T(1024)S(1)} %get-tuple-element.106), channel_id=1, replica_groups=mesh['dp'=8,'tensor'=4] {'dp'}, use_global_device_ids=true, to_apply=%region_27.28 | all-reduce | flops 2880 | bytes 23040 | tf_op jit(solution)/shard_map/psum | solution.py:290
  847.7 59.1 %reduce-scatter.30.cloned.1.call-done = f32[160,1280]{1,0:T(8,128)} async-done(((f32[1280,1280]{1,0:T(8,128)}), f32[160,1280]{1,0:T(8,128)}) %reduce-scatter.30.cloned.1.call-update) | async-done | bytes 819216 | tf_op jit(solution)/shard_map/reduce_scatter | solution.py:248
  906.8 66.9 %reduce-scatter.32.cloned.1.call-done = f32[160,1280]{1,0:T(8,128)} async-done(((f32[1280,1280]{1,0:T(8,128)}), f32[160,1280]{1,0:T(8,128)}) %reduce-scatter.32.cloned.1.call-update) | async-done | bytes 819216 | tf_op jit(solution)/shard_map/reduce_scatter | solution.py:249
  973.7 43.9 %reduce-scatter.34.cloned.1.call-done = f32[160,320]{1,0:T(8,128)} async-done(((f32[1280,320]{1,0:T(8,128)}), f32[160,320]{1,0:T(8,128)}) %reduce-scatter.34.cloned.1.call-update) | async-done | bytes 204816
  1017.6 44.1 %reduce-scatter.36.cloned.1.call-done = f32[160,320]{1,0:T(8,128)} async-done(((f32[1280,320]{1,0:T(8,128)}), f32[160,320]{1,0:T(8,128)}) %reduce-scatter.36.cloned.1.call-update) | async-done | bytes 204816
  1061.7 43.9 %reduce-scatter.38.cloned.1.call-done = f32[160,320]{1,0:T(8,128)} async-done(((f32[1280,320]{1,0:T(8,128)}), f32[160,320]{1,0:T(8,128)}) %reduce-scatter.38.cloned.1.call-update) | async-done | bytes 204816
  1105.6 44.1 %reduce-scatter.26.cloned.1.call-done = f32[160,320]{1,0:T(8,128)} async-done(((f32[1280,320]{1,0:T(8,128)}), f32[160,320]{1,0:T(8,128)}) %reduce-scatter.26.cloned.1.call-update) | async-done | bytes 204816 | tf_op jit(solution)/shard_map/reduce_scatter | solution.py:288
  (244 shorter events, 76.4 us)
Async XLA Ops:
  8.0 13.7 %copy-start.50 = (bf16[160,320]{1,0:T(8,128)(2,1)S(1)}, bf16[160,320]{1,0:T(8,128)(2,1)}, u32[]{:S(2)}) copy-start(bf16[160,320]{1,0:T(8,128)(2,1)} %param.28) | copy-start | bytes 307204
  8.0 25.3 %copy-start.51 = (bf16[160,320]{1,0:T(8,128)(2,1)S(1)}, bf16[160,320]{1,0:T(8,128)(2,1)}, u32[]{:S(2)}) copy-start(bf16[160,320]{1,0:T(8,128)(2,1)} %param.27) | copy-start | bytes 307204
  8.0 59.9 %all-gather.8.cloned.1.call-start = ((), (), s32[]{:S(2)}) async-start(), calls=%async_computation.11 | async-start | bytes 3276800 | tf_op jit(solution)/shard_map/all_gather | solution.py:188
  8.8 189.7 %reduce-scatter.18.cloned.1.call-start = ((), (), s32[]{:S(2)}) async-start(), calls=%async_computation.12 | async-start | bytes 6553600 | tf_op jit(solution)/shard_map/reduce_scatter | solution.py:206
  9.0 35.8 %copy-start.52 = (bf16[160,320]{1,0:T(8,128)(2,1)S(1)}, bf16[160,320]{1,0:T(8,128)(2,1)}, u32[]{:S(2)}) copy-start(bf16[160,320]{1,0:T(8,128)(2,1)} %param.30) | copy-start | bytes 307204
  21.8 70.9 %copy-start.24 = (bf16[1280,320]{1,0:T(8,128)(2,1)}, bf16[1280,320]{1,0:T(8,128)(2,1)S(1)}, u32[]{:S(2)}) copy-start(bf16[1280,320]{1,0:T(8,128)(2,1)S(1)} %all_gather.41) | copy-start | bytes 2457604
  83.3 4.2 copy-start.10
  87.5 6.3 copy-start.33
  87.5 6.3 copy-start.35
  89.5 6.5 copy-start
  93.8 5.1 copy-start.42
  94.9 4.1 copy-start.1
  105.8 94.3 %copy-start.49 = (f32[1280]{0:T(1024)S(1)}, f32[1280]{0:T(1024)}, u32[]{:S(2)}) copy-start(f32[1280]{0:T(1024)} %param.37) | copy-start | bytes 15364
  105.8 98.7 %all-gather.14.cloned.1.call-start = ((), (), s32[]{:S(2)}) async-start(), calls=%async_computation.15 | async-start | bytes 3686400 | tf_op jit(solution)/shard_map/all_gather | solution.py:166
  106.4 151.4 %all-gather.10.cloned.1.call-start = ((), (), s32[]{:S(2)}) async-start(), calls=%async_computation.13 | async-start | bytes 3276800 | tf_op jit(solution)/shard_map/all_gather | solution.py:214
  202.8 88.0 %all-gather.12.cloned.1.call-start = ((), (), s32[]{:S(2)}) async-start(), calls=%async_computation.14 | async-start | bytes 3686400 | tf_op jit(solution)/shard_map/all_gather | solution.py:165
  203.4 122.0 %all-gather.16.cloned.1.call-start = ((), (), s32[]{:S(2)}) async-start(), calls=%async_computation.16 | async-start | bytes 3686400 | tf_op jit(solution)/shard_map/all_gather | solution.py:167
  204.1 86.7 %copy-start.57 = (f32[1280]{0:T(1024)S(1)}, f32[1280]{0:T(1024)}, u32[]{:S(2)}) copy-start(f32[1280]{0:T(1024)} %param.35) | copy-start | bytes 15364
  204.1 86.7 %copy-start.58 = (f32[1280]{0:T(1024)S(1)}, f32[1280]{0:T(1024)}, u32[]{:S(2)}) copy-start(f32[1280]{0:T(1024)} %param.36) | copy-start | bytes 15364
  204.1 223.9 %reduce-scatter.20.cloned.1.call-start = ((), (), s32[]{:S(2)}) async-start(), calls=%async_computation.17 | async-start | bytes 6553600 | tf_op jit(solution)/shard_map/reduce_scatter | solution.py:221
  334.1 95.6 %copy-start.48 = (f32[1280]{0:T(1024)S(1)}, f32[1280]{0:T(1024)}, u32[]{:S(2)}) copy-start(f32[1280]{0:T(1024)} %param.38) | copy-start | bytes 15364
  334.1 155.9 %all-gather.18.cloned.1.call-start = ((), (), s32[]{:S(2)}) async-start(), calls=%async_computation.18 | async-start | bytes 3276800 | tf_op jit(solution)/shard_map/all_gather | solution.py:231
  434.9 168.5 %reduce-scatter.22.cloned.1.call-start = ((), (), s32[]{:S(2)}) async-start(), calls=%async_computation.19 | async-start | bytes 6553600 | tf_op jit(solution)/shard_map/reduce_scatter | solution.py:243
  490.0 11.1 copy-start.55
  501.1 3.6 copy-start.60
  501.1 3.8 copy-start.59
  501.1 4.4 copy-start.54
  510.9 154.7 %all-gather.20.cloned.1.call-start = ((), (), s32[]{:S(2)}) async-start(), calls=%async_computation.20 | async-start | bytes 3276800 | tf_op jit(solution)/shard_map/all_gather | solution.py:255
  609.4 56.2 %copy-start.30 = (bf16[1280,320]{1,0:T(8,128)(2,1)S(1)}, bf16[1280,320]{1,0:T(8,128)(2,1)}, u32[]{:S(2)}) copy-start(bf16[1280,320]{1,0:T(8,128)(2,1)} %all_gather.44) | copy-start | bytes 2457604
  610.5 58.6 %copy-start.43 = (bf16[512,320]{0,1:T(8,128)(2,1)S(1)}, bf16[512,320]{0,1:T(8,128)(2,1)}, u32[]{:S(2)}) copy-start(bf16[512,320]{0,1:T(8,128)(2,1)} %copy-done.42) | copy-start | bytes 983044
  610.5 234.9 %reduce-scatter.24.cloned.1.call-start = ((), (), s32[]{:S(2)}) async-start(), calls=%async_computation.21 | async-start | bytes 3276800 | tf_op jit(solution)/shard_map/reduce_scatter | solution.py:281
  669.1 4.5 copy-start.40
  669.1 10.7 slice-start
  669.1 10.7 slice-start.1
  673.7 4.2 copy-start.36
  673.7 6.1 slice-start.2
  683.9 3.3 copy-start.15
  695.2 7.7 slice-start.3
  705.3 6.0 copy-start.28
  714.6 3.9 copy-start.25
  721.8 125.9 %reduce-scatter.28.cloned.1.call-start = ((), (), s32[]{:S(2)}) async-start(), calls=%async_computation.23 | async-start | bytes 7372800 | tf_op jit(solution)/shard_map/reduce_scatter | solution.py:247
  730.8 176.0 %reduce-scatter.30.cloned.1.call-start = ((), (), s32[]{:S(2)}) async-start(), calls=%async_computation.24 | async-start | bytes 7372800 | tf_op jit(solution)/shard_map/reduce_scatter | solution.py:248
  740.7 233.0 %reduce-scatter.32.cloned.1.call-start = ((), (), s32[]{:S(2)}) async-start(), calls=%async_computation.25 | async-start | bytes 7372800 | tf_op jit(solution)/shard_map/reduce_scatter | solution.py:249
  749.6 268.0 %reduce-scatter.34.cloned.1.call-start = ((), (), s32[]{:S(2)}) async-start(), calls=%async_computation.26 | async-start | bytes 2211840
  757.5 304.2 %reduce-scatter.36.cloned.1.call-start = ((), (), s32[]{:S(2)}) async-start(), calls=%async_computation.27 | async-start | bytes 2211840
  765.3 340.3 %reduce-scatter.38.cloned.1.call-start = ((), (), s32[]{:S(2)}) async-start(), calls=%async_computation.28 | async-start | bytes 2211840
  773.1 376.6 %reduce-scatter.26.cloned.1.call-start = ((), (), s32[]{:S(2)}) async-start(), calls=%async_computation.22 | async-start | bytes 2211840 | tf_op jit(solution)/shard_map/reduce_scatter | solution.py:288
  820.0 25.4 %copy-start.13 = (f32[256,1280]{1,0:T(8,128)S(1)}, f32[256,1280]{1,0:T(8,128)}, u32[]{:S(2)}) copy-start(f32[256,1280]{1,0:T(8,128)} %copy-done.12) | copy-start | bytes 3932164
  (36 other events, 56.8 us)
Sparse Core Ops, SparseCore 0:
  10.4 57.4 all-gather.7
  105.9 92.5 reduce-scatter.17
  334.2 93.7 reduce-scatter.19
  511.0 92.3 reduce-scatter.21
Sparse Core Ops, SparseCore 1:
  108.2 31.4 all-gather.13
  202.9 54.9 all-gather.9
  259.6 31.2 all-gather.11
  292.7 32.6 all-gather.15
  435.0 54.9 all-gather.17
  610.6 54.9 all-gather.19
  721.9 50.8 reduce-scatter.23
  776.6 63.3 reduce-scatter.27
  843.9 62.9 reduce-scatter.29
  910.8 62.8 reduce-scatter.31
  977.6 40.0 reduce-scatter.33
  1021.6 40.0 reduce-scatter.35
  1065.6 40.0 reduce-scatter.37
  1109.6 40.0 reduce-scatter.25
where the time goes:
time: 1160 us
  waiting for transfers between devices  805 us (69%)
  matrix products  153 us (13%)
  blocking collectives  112 us (10%)
  other arithmetic  43.9 us (4%)
  local copies, waits for them, and re-layouts  24.4 us (2%)
  between operations  16.9 us (1%)
    unnamed x21, waiting for transfers between devices  135 us
    reduce_scatter x1, waiting for transfers between devices, on_device(): lax.psum_scatter(contract_cols(hidden_low, down_w), 'tensor', scatter_dim...  93.9 us
    reduce_scatter x1, waiting for transfers between devices, on_device(): lax.psum_scatter(g_mid_part, 'tensor', scatter_dimension=0, tiled=True)  92.5 us
    reduce_scatter x1, waiting for transfers between devices, on_device(): lax.psum_scatter(contract_cols(attended_low, out_w), 'tensor', scatter_di...  92.1 us
    reduce_scatter x1, waiting for transfers between devices, on_device(): lax.psum_scatter(down_grad, 'dp', scatter_dimension=0, tiled=True)  66.9 us
    reduce_scatter x1, waiting for transfers between devices, on_device(): lax.psum_scatter(gate_grad, 'dp', scatter_dimension=0, tiled=True)  59.1 us
    all_gather x1, waiting for transfers between devices, on_device(): g_attn_whole = lax.all_gather(g_attn_low, 'tensor', axis=0, tiled=True)  54.8 us
    all_gather x1, waiting for transfers between devices, on_device(): g_mlp_whole = lax.all_gather(g_mlp_low, 'tensor', axis=0, tiled=True)  54.5 us
  transfers between devices with their start and end apart: 18, of which 15 were waited for; matrix products, arithmetic and copies ran while one was open for 7% of the time, Pallas kernels for 0%

commit v1 on v0

--- a/solution.py
+++ b/solution.py
@@ -6,6 +6,27 @@
 HEAD_DIM = 64
 HIGH = lax.Precision.HIGHEST
 EPS = 1e-06
+
+
+def ring_gather(x, axis, dim):
+    devices, index, span = (lax.axis_size(axis), lax.axis_index(axis), x.shape[dim])
+    upward = [(i, (i + 1) % devices) for i in range(devices)]
+    behind = [(i, (i - 1) % devices) for i in range(devices)]
+    out = jnp.zeros((*x.shape[:dim], devices * span, *x.shape[dim + 1 :]), x.dtype)
+    out = lax.dynamic_update_slice_in_dim(out, x, index * span, axis=dim)
+    from_left = from_right = x
+    half = devices // 2
+    for hop in range(1, half + 1):
+        from_left = lax.ppermute(from_left, axis, upward)
+        out = lax.dynamic_update_slice_in_dim(
+            out, from_left, (index - hop) % devices * span, axis=dim
+        )
+        if hop < devices - half:
+            from_right = lax.ppermute(from_right, axis, behind)
+            out = lax.dynamic_update_slice_in_dim(
+                out, from_right, (index + hop) % devices * span, axis=dim
+            )
+    return out
 
 
 def unit_rows(value):
@@ -162,7 +183,7 @@
 
 def gather_feedforward(w_up, w_gate, w_down):
     return (
-        lax.all_gather(w_up, "dp", axis=0, tiled=True),
+        ring_gather(w_up, "dp", 0),
         lax.all_gather(w_gate, "dp", axis=0, tiled=True),
         lax.all_gather(w_down, "dp", axis=0, tiled=True),
     )

time: 1160 us -> 1130 us (0.974)
  waiting for transfers between devices: 805 us -> 758 us
    all_gather x1, waiting for transfers between devices: 53.4 us -> 10.2 us  [on_device(): mid_whole = lax.all_gather(mid_low, 'tensor', axis=0, tiled=True)]
    ppermute x0 -> x7, waiting for transfers between devices: none -> 25.7 us  [the longest x4 25.7 us: ring_gather(): from_left = lax.ppermute(from_left, axis, upward)]
    all_gather x1 -> x0, waiting for transfers between devices: 24.5 us -> none  [gather_feedforward(): lax.all_gather(w_up, 'dp', axis=0, tiled=True)]
    unnamed x21 -> x20, waiting for transfers between devices: 135 us -> 134 us
  transfers between devices with their start and end apart: 18 -> 24, of which waited for: 15 -> 18; matrix products, arithmetic and copies ran while one was open for 7% -> 8% of each run, Pallas kernels for 0% -> 0%
where the time goes in v1:
time: 1130 us
  waiting for transfers between devices  758 us (67%)
  matrix products  150 us (13%)
  blocking collectives  113 us (10%)
  other arithmetic  45.5 us (4%)
  local copies, waits for them, and re-layouts  32 us (3%)
  between operations  17.1 us (2%)
    unnamed x20, waiting for transfers between devices  134 us
    reduce_scatter x1, waiting for transfers between devices, on_device(): lax.psum_scatter(contract_cols(hidden_low, down_w), 'tensor', scatter_dim...  93.9 us
    reduce_scatter x1, waiting for transfers between devices, on_device(): lax.psum_scatter(g_mid_part, 'tensor', scatter_dimension=0, tiled=True)  92.4 us
    reduce_scatter x1, waiting for transfers between devices, on_device(): lax.psum_scatter(contract_cols(attended_low, out_w), 'tensor', scatter_di...  92.1 us
    reduce_scatter x1, waiting for transfers between devices, on_device(): lax.psum_scatter(down_grad, 'dp', scatter_dimension=0, tiled=True)  67 us
    reduce_scatter x1, waiting for transfers between devices, on_device(): lax.psum_scatter(gate_grad, 'dp', scatter_dimension=0, tiled=True)  62.4 us
    all_gather x1, waiting for transfers between devices, on_device(): g_attn_whole = lax.all_gather(g_attn_low, 'tensor', axis=0, tiled=True)  55.2 us
    all_gather x1, waiting for transfers between devices, on_device(): g_mlp_whole = lax.all_gather(g_mlp_low, 'tensor', axis=0, tiled=True)  54.5 us
  transfers between devices with their start and end apart: 24, of which 18 were waited for; matrix products, arithmetic and copies ran while one was open for 8% of the time, Pallas kernels for 0%

profile of v1, /device:TPU:0, one launch (start us, length us, event | category | flops | bytes accessed | tf_op | source)
XLA Modules:
  0.0 1125.6 jit_solution(6600747210393966046)
XLA Ops:
  9.0 12.7 %all_gather.37 = bf16[1280,320]{1,0:T(8,128)(2,1)S(1)} all-gather(bf16[160,320]{1,0:T(8,128)(2,1)} %param.29), channel_id=1, replica_groups=mesh['dp'=8,'tensor'=4] {'dp'}, dimensions={0}, use_global_device_ids=true | all-gather | bytes 921600 | tf_op jit(solution)/shard_map/all_gather | solution.py:179
  21.6 12.6 %all_gather.39 = bf16[1280,320]{1,0:T(8,128)(2,1)} all-gather(bf16[160,320]{1,0:T(8,128)(2,1)} %param.28), channel_id=1, replica_groups=mesh['dp'=8,'tensor'=4] {'dp'}, dimensions={0}, use_global_device_ids=true | all-gather | bytes 921600 | tf_op jit(solution)/shard_map/all_gather | solution.py:178
  34.2 11.5 %all_gather.38 = bf16[1280,320]{1,0:T(8,128)(2,1)} all-gather(bf16[160,320]{1,0:T(8,128)(2,1)S(1)} %copy-done.50), channel_id=1, replica_groups=mesh['dp'=8,'tensor'=4] {'dp'}, dimensions={0}, use_global_device_ids=true | all-gather | bytes 921600 | tf_op jit(solution)/shard_map/all_gather | solution.py:177
  45.7 11.3 %all_gather.40 = bf16[1280,320]{1,0:T(8,128)(2,1)} all-gather(bf16[160,320]{1,0:T(8,128)(2,1)S(1)} %copy-done.51), channel_id=1, replica_groups=mesh['dp'=8,'tensor'=4] {'dp'}, dimensions={0}, use_global_device_ids=true | all-gather | bytes 921600 | tf_op jit(solution)/shard_map/all_gather | solution.py:180
  57.4 10.5 all-gather.7.cloned.1.call-done
  67.9 3.0 fusion.125
  74.3 6.5 fusion.20
  89.5 3.1 exponential_reduce_fusion
  101.4 3.9 fusion.126
  105.9 92.1 %reduce-scatter.18.cloned.1.call-done = f32[256,1280]{1,0:T(8,128)} async-done(((f32[1024,1280]{1,0:T(8,128)}), f32[256,1280]{1,0:T(8,128)}) %reduce-scatter.18.cloned.1.call-update) | async-done | bytes 1310736 | tf_op jit(solution)/shard_map/reduce_scatter | solution.py:227
  208.5 5.9 collective-permute-done
  220.6 5.4 collective-permute-done.2
  230.3 7.8 collective-permute-done.4
  239.9 6.7 collective-permute-done.6
  247.3 10.2 all-gather.9.cloned.1.call-done
  257.5 6.4 fusion.127
  266.3 8.1 multiply_convert_fusion.4
  274.3 16.2 %all-gather.13.cloned.1.call-done = bf16[1280,1280]{1,0:T(8,128)(2,1)} async-done(((bf16[160,1280]{1,0:T(8,128)(2,1)}), bf16[1280,1280]{1,0:T(8,128)(2,1)}) %all-gather.13.cloned.1.call-update) | async-done | bytes 3276816 | tf_op jit(solution)/shard_map/all_gather | solution.py:188
  290.5 8.7 fusion.128
  299.3 93.9 %reduce-scatter.20.cloned.1.call-done = f32[256,1280]{1,0:T(8,128)} async-done(((f32[1024,1280]{1,0:T(8,128)}), f32[256,1280]{1,0:T(8,128)}) %reduce-scatter.20.cloned.1.call-update) | async-done | bytes 1310736 | tf_op jit(solution)/shard_map/reduce_scatter | solution.py:242
  401.3 54.5 %all-gather.15.cloned.1.call-done = bf16[1024,1280]{1,0:T(8,128)(2,1)} async-done(((bf16[256,1280]{1,0:T(8,128)(2,1)}), bf16[1024,1280]{1,0:T(8,128)(2,1)}) %all-gather.15.cloned.1.call-update) | async-done | bytes 2621456 | tf_op jit(solution)/shard_map/all_gather | solution.py:252
  455.8 11.1 multiply_reduce_fusion.1
  466.9 3.6 fusion.69
  470.5 7.3 convolution_add_fusion
  477.9 92.4 %reduce-scatter.22.cloned.1.call-done = f32[256,1280]{1,0:T(8,128)} async-done(((f32[1024,1280]{1,0:T(8,128)}), f32[256,1280]{1,0:T(8,128)}) %reduce-scatter.22.cloned.1.call-update) | async-done | bytes 1310736 | tf_op jit(solution)/shard_map/reduce_scatter | solution.py:264
  577.6 55.2 %all-gather.17.cloned.1.call-done = bf16[1024,1280]{1,0:T(8,128)(2,1)} async-done(((bf16[256,1280]{1,0:T(8,128)(2,1)}), bf16[1024,1280]{1,0:T(8,128)(2,1)}) %all-gather.17.cloned.1.call-update) | async-done | bytes 2621456 | tf_op jit(solution)/shard_map/all_gather | solution.py:276
  636.4 4.5 multiply_reduce_fusion.3
  640.9 4.2 multiply_convert_fusion.1
  647.3 3.9 multiply_reduce_fusion
  651.2 3.3 multiply_convert_fusion
  662.3 7.2 fusion.35
  672.4 6.0 fusion.24
  685.5 3.3 add_convert_fusion
  688.9 8.8 fusion.132
  698.0 9.7 fusion.68
  707.8 8.8 fusion.133
  717.7 4.0 convolution_bitcast_fusion.2
  724.7 3.9 convolution_bitcast_fusion.1
  731.6 3.9 convolution_bitcast_fusion
  738.5 4.6 fusion.131
  743.1 39.7 %all-reduce.2 = (f32[1280]{0:T(1024)}, f32[1280]{0:T(1024)}) all-reduce(f32[1280]{0:T(1024)S(1)} %get-tuple-element.110, f32[1280]{0:T(1024)S(1)} %get-tuple-element.108), channel_id=1, replica_groups=mesh['dp'=8,'tensor'=4] {'dp','tensor'}, use_global_device_ids=true, to_apply=%region_33.34 | all-reduce | flops 2560 | bytes 20480 | tf_op jit(solution)/shard_map/psum | solution.py:314
  784.7 25.1 %all-reduce.3 = (f32[320]{0:T(512)}, f32[1280]{0:T(1024)}, f32[1280]{0:T(1024)}) all-reduce(f32[320]{0:T(512)S(1)} %add.348, f32[1280]{0:T(1024)S(1)} %get-tuple-element.107, f32[1280]{0:T(1024)S(1)} %get-tuple-element.106), channel_id=1, replica_groups=mesh['dp'=8,'tensor'=4] {'dp'}, use_global_device_ids=true, to_apply=%region_27.28 | all-reduce | flops 2880 | bytes 23040 | tf_op jit(solution)/shard_map/psum | solution.py:311
  812.1 62.4 %reduce-scatter.30.cloned.1.call-done = f32[160,1280]{1,0:T(8,128)} async-done(((f32[1280,1280]{1,0:T(8,128)}), f32[160,1280]{1,0:T(8,128)}) %reduce-scatter.30.cloned.1.call-update) | async-done | bytes 819216 | tf_op jit(solution)/shard_map/reduce_scatter | solution.py:269
  874.4 67.0 %reduce-scatter.32.cloned.1.call-done = f32[160,1280]{1,0:T(8,128)} async-done(((f32[1280,1280]{1,0:T(8,128)}), f32[160,1280]{1,0:T(8,128)}) %reduce-scatter.32.cloned.1.call-update) | async-done | bytes 819216 | tf_op jit(solution)/shard_map/reduce_scatter | solution.py:270
  941.5 44.2 %reduce-scatter.34.cloned.1.call-done = f32[160,320]{1,0:T(8,128)} async-done(((f32[1280,320]{1,0:T(8,128)}), f32[160,320]{1,0:T(8,128)}) %reduce-scatter.34.cloned.1.call-update) | async-done | bytes 204816
  985.6 44.0 %reduce-scatter.36.cloned.1.call-done = f32[160,320]{1,0:T(8,128)} async-done(((f32[1280,320]{1,0:T(8,128)}), f32[160,320]{1,0:T(8,128)}) %reduce-scatter.36.cloned.1.call-update) | async-done | bytes 204816
  1029.7 44.2 %reduce-scatter.38.cloned.1.call-done = f32[160,320]{1,0:T(8,128)} async-done(((f32[1280,320]{1,0:T(8,128)}), f32[160,320]{1,0:T(8,128)}) %reduce-scatter.38.cloned.1.call-update) | async-done | bytes 204816
  1073.8 44.0 %reduce-scatter.26.cloned.1.call-done = f32[160,320]{1,0:T(8,128)} async-done(((f32[1280,320]{1,0:T(8,128)}), f32[160,320]{1,0:T(8,128)}) %reduce-scatter.26.cloned.1.call-update) | async-done | bytes 204816 | tf_op jit(solution)/shard_map/reduce_scatter | solution.py:309
  (264 shorter events, 101.4 us)
Async XLA Ops:
  8.0 26.2 %copy-start.50 = (bf16[160,320]{1,0:T(8,128)(2,1)S(1)}, bf16[160,320]{1,0:T(8,128)(2,1)}, u32[]{:S(2)}) copy-start(bf16[160,320]{1,0:T(8,128)(2,1)} %param.27) | copy-start | bytes 307204
  8.0 37.7 %copy-start.51 = (bf16[160,320]{1,0:T(8,128)(2,1)S(1)}, bf16[160,320]{1,0:T(8,128)(2,1)}, u32[]{:S(2)}) copy-start(bf16[160,320]{1,0:T(8,128)(2,1)} %param.30) | copy-start | bytes 307204
  8.0 59.9 %all-gather.7.cloned.1.call-start = ((), (), s32[]{:S(2)}) async-start(), calls=%async_computation.11 | async-start | bytes 3276800 | tf_op jit(solution)/shard_map/all_gather | solution.py:209
  8.8 189.2 %reduce-scatter.18.cloned.1.call-start = ((), (), s32[]{:S(2)}) async-start(), calls=%async_computation.12 | async-start | bytes 6553600 | tf_op jit(solution)/shard_map/reduce_scatter | solution.py:227
  21.6 71.0 %copy-start.23 = (bf16[1280,320]{1,0:T(8,128)(2,1)}, bf16[1280,320]{1,0:T(8,128)(2,1)S(1)}, u32[]{:S(2)}) copy-start(bf16[1280,320]{1,0:T(8,128)(2,1)S(1)} %all_gather.37) | copy-start | bytes 2457604
  83.2 4.2 copy-start.9
  87.4 6.3 copy-start.32
  87.5 6.3 copy-start.34
  89.5 6.5 copy-start
  93.8 5.1 copy-start.41
  105.3 94.2 %copy-start.49 = (f32[1280]{0:T(1024)S(1)}, f32[1280]{0:T(1024)}, u32[]{:S(2)}) copy-start(f32[1280]{0:T(1024)} %param.37) | copy-start | bytes 15364
  105.3 142.0 %all-gather.11.cloned.1.call-start = ((), (), s32[]{:S(2)}) async-start(), calls=%async_computation.14 | async-start | bytes 3686400 | tf_op jit(solution)/shard_map/all_gather | solution.py:187
  105.9 151.6 %all-gather.9.cloned.1.call-start = ((), (), s32[]{:S(2)}) async-start(), calls=%async_computation.13 | async-start | bytes 3276800 | tf_op jit(solution)/shard_map/all_gather | solution.py:235
  202.5 88.0 %all-gather.13.cloned.1.call-start = ((), (), s32[]{:S(2)}) async-start(), calls=%async_computation.15 | async-start | bytes 3686400 | tf_op jit(solution)/shard_map/all_gather | solution.py:188
  203.1 190.1 %reduce-scatter.20.cloned.1.call-start = ((), (), s32[]{:S(2)}) async-start(), calls=%async_computation.16 | async-start | bytes 6553600 | tf_op jit(solution)/shard_map/reduce_scatter | solution.py:242
  203.1 11.2 collective-permute-start
  203.2 11.2 collective-permute-start.1
  214.4 11.7 %collective-permute-start.2 = (bf16[160,1280]{1,0:T(8,128)(2,1)}, bf16[160,1280]{1,0:T(8,128)(2,1)S(1)}, u32[]{:S(2)}, u32[]{:S(2)}) collective-permute-start(bf16[160,1280]{1,0:T(8,128)(2,1)} %collective-permute-done), channel_id=1, source_target_pairs={{0,4},{4,8},{8,12},{12,16},{16,20},{20,24},{24,28},{28,0},{1,5},{5... | collective-permute-start | bytes 1228808 | tf_op jit(solution)/shard_map/ppermute | solution.py:20
  214.4 11.7 %collective-permute-start.3 = (bf16[160,1280]{1,0:T(8,128)(2,1)}, bf16[160,1280]{1,0:T(8,128)(2,1)S(1)}, u32[]{:S(2)}, u32[]{:S(2)}) collective-permute-start(bf16[160,1280]{1,0:T(8,128)(2,1)} %collective-permute-done.1), channel_id=1, source_target_pairs={{0,28},{4,0},{8,4},{12,8},{16,12},{20,16},{24,20},{28,24},{1,29},{... | collective-permute-start | bytes 1228808 | tf_op jit(solution)/shard_map/ppermute | solution.py:25
  226.1 12.0 %collective-permute-start.4 = (bf16[160,1280]{1,0:T(8,128)(2,1)S(1)}, bf16[160,1280]{1,0:T(8,128)(2,1)S(1)}, u32[]{:S(2)}, u32[]{:S(2)}) collective-permute-start(bf16[160,1280]{1,0:T(8,128)(2,1)S(1)} %collective-permute-done.2), channel_id=1, source_target_pairs={{0,4},{4,8},{8,12},{12,16},{16,20},{20,24},{24,28},{28,0},{1,5},{5... | collective-permute-start | bytes 1228808 | tf_op jit(solution)/shard_map/ppermute | solution.py:20
  226.1 13.0 %collective-permute-start.5 = (bf16[160,1280]{1,0:T(8,128)(2,1)S(1)}, bf16[160,1280]{1,0:T(8,128)(2,1)S(1)}, u32[]{:S(2)}, u32[]{:S(2)}) collective-permute-start(bf16[160,1280]{1,0:T(8,128)(2,1)S(1)} %collective-permute-done.3), channel_id=1, source_target_pairs={{0,28},{4,0},{8,4},{12,8},{16,12},{20,16},{24,20},{28,24},{1,29},{... | collective-permute-start | bytes 1228808 | tf_op jit(solution)/shard_map/ppermute | solution.py:25
  238.0 8.5 collective-permute-start.6
  247.3 18.9 %copy-start.56 = (f32[1280]{0:T(1024)S(1)}, f32[1280]{0:T(1024)}, u32[]{:S(2)}) copy-start(f32[1280]{0:T(1024)} %param.35) | copy-start | bytes 15364
  247.3 18.9 %copy-start.57 = (f32[1280]{0:T(1024)S(1)}, f32[1280]{0:T(1024)}, u32[]{:S(2)}) copy-start(f32[1280]{0:T(1024)} %param.36) | copy-start | bytes 15364
  257.5 8.8 copy-start.55
  299.2 95.5 %copy-start.48 = (f32[1280]{0:T(1024)S(1)}, f32[1280]{0:T(1024)}, u32[]{:S(2)}) copy-start(f32[1280]{0:T(1024)} %param.38) | copy-start | bytes 15364
  299.2 156.6 %all-gather.15.cloned.1.call-start = ((), (), s32[]{:S(2)}) async-start(), calls=%async_computation.17 | async-start | bytes 3276800 | tf_op jit(solution)/shard_map/all_gather | solution.py:252
  400.8 169.5 %reduce-scatter.22.cloned.1.call-start = ((), (), s32[]{:S(2)}) async-start(), calls=%async_computation.18 | async-start | bytes 6553600 | tf_op jit(solution)/shard_map/reduce_scatter | solution.py:264
  455.8 11.1 copy-start.53
  477.9 154.9 %all-gather.17.cloned.1.call-start = ((), (), s32[]{:S(2)}) async-start(), calls=%async_computation.19 | async-start | bytes 3276800 | tf_op jit(solution)/shard_map/all_gather | solution.py:276
  575.1 57.6 %copy-start.29 = (bf16[1280,320]{1,0:T(8,128)(2,1)S(1)}, bf16[1280,320]{1,0:T(8,128)(2,1)}, u32[]{:S(2)}) copy-start(bf16[1280,320]{1,0:T(8,128)(2,1)} %all_gather.40) | copy-start | bytes 2457604
  577.4 59.0 %copy-start.42 = (bf16[512,320]{0,1:T(8,128)(2,1)S(1)}, bf16[512,320]{0,1:T(8,128)(2,1)}, u32[]{:S(2)}) copy-start(bf16[512,320]{0,1:T(8,128)(2,1)} %copy-done.41) | copy-start | bytes 983044
  577.4 232.4 %reduce-scatter.24.cloned.1.call-start = ((), (), s32[]{:S(2)}) async-start(), calls=%async_computation.20 | async-start | bytes 3276800 | tf_op jit(solution)/shard_map/reduce_scatter | solution.py:302
  636.4 4.5 copy-start.39
  636.4 10.7 slice-start
  636.4 10.7 slice-start.1
  640.9 4.2 copy-start.35
  640.9 6.1 slice-start.2
  662.3 7.7 slice-start.3
  672.4 6.0 copy-start.27
  688.9 123.2 %reduce-scatter.28.cloned.1.call-start = ((), (), s32[]{:S(2)}) async-start(), calls=%async_computation.22 | async-start | bytes 7372800 | tf_op jit(solution)/shard_map/reduce_scatter | solution.py:268
  697.8 176.6 %reduce-scatter.30.cloned.1.call-start = ((), (), s32[]{:S(2)}) async-start(), calls=%async_computation.23 | async-start | bytes 7372800 | tf_op jit(solution)/shard_map/reduce_scatter | solution.py:269
  707.8 233.7 %reduce-scatter.32.cloned.1.call-start = ((), (), s32[]{:S(2)}) async-start(), calls=%async_computation.24 | async-start | bytes 7372800 | tf_op jit(solution)/shard_map/reduce_scatter | solution.py:270
  716.7 269.0 %reduce-scatter.34.cloned.1.call-start = ((), (), s32[]{:S(2)}) async-start(), calls=%async_computation.25 | async-start | bytes 2211840
  724.6 305.0 %reduce-scatter.36.cloned.1.call-start = ((), (), s32[]{:S(2)}) async-start(), calls=%async_computation.26 | async-start | bytes 2211840
  731.5 342.3 %reduce-scatter.38.cloned.1.call-start = ((), (), s32[]{:S(2)}) async-start(), calls=%async_computation.27 | async-start | bytes 2211840
  738.4 379.5 %reduce-scatter.26.cloned.1.call-start = ((), (), s32[]{:S(2)}) async-start(), calls=%async_computation.21 | async-start | bytes 2211840 | tf_op jit(solution)/shard_map/reduce_scatter | solution.py:309
  784.5 25.3 %copy-start.12 = (f32[256,1280]{1,0:T(8,128)S(1)}, f32[256,1280]{1,0:T(8,128)}, u32[]{:S(2)}) copy-start(f32[256,1280]{1,0:T(8,128)} %copy-done.11) | copy-start | bytes 3932164
  (42 other events, 88.8 us)
Sparse Core Ops, SparseCore 0:
  10.4 57.4 all-gather.6
  105.4 92.5 reduce-scatter.17
  299.3 93.7 reduce-scatter.19
  577.5 55.2 all-gather.16
  689.0 51.0 reduce-scatter.23
  743.9 63.5 reduce-scatter.27
  811.5 62.8 reduce-scatter.29
  878.5 62.9 reduce-scatter.31
  945.5 40.1 reduce-scatter.33
  989.5 40.1 reduce-scatter.35
  1033.6 40.1 reduce-scatter.37
  1077.7 40.1 reduce-scatter.25
Sparse Core Ops, SparseCore 1:
  107.7 31.4 all-gather.10
  202.6 54.9 all-gather.8
  259.3 31.2 all-gather.12
  400.8 54.9 all-gather.14
  477.9 92.3 reduce-scatter.21
